TPU v7x, 512 devices: a whole 4x8x8 slice. The times are simulated.
512 devices in a mesh: batch: 64 (over x, z, y_hi), space: 8 (over y_lo, core).
Axes of the slice: x: 4, y: 8 (y_hi: 2, y_lo: 4; y = y_hi * 4 + y_lo), z: 8, core: 2. Of those that a mesh axis runs over, the one named last changes fastest.
Arguments:
- latents: float32 [64, 32, 64, 4], P('batch', 'space'), may hold values from -16 to 16
- noise_draw: float32 [64, 32, 64, 4], P('batch', 'space'), may hold values from -5 to 5
- timesteps: int32 [64], P('batch'), may hold values from 200 to 799
- inlet_conv: bfloat16 [36, 320], replicated, may hold values from -1 to 1
- time_first: bfloat16 [320, 1280], P(None, 'batch'), may hold values from -0.3125 to 0.3125
- time_first_bias: float32 [1280], replicated, may hold values from -4 to 4
- time_second: bfloat16 [1280, 320], P(None, 'batch'), may hold values from -0.3125 to 0.3125
- time_second_bias: float32 [320], replicated, may hold values from -4 to 4
- conv_first: bfloat16 [2880, 320], P(None, 'batch'), may hold values from -0.109375 to 0.109375
- conv_second: bfloat16 [2880, 320], P(None, 'batch'), may hold values from -0.109375 to 0.109375
- proj_inner: bfloat16 [320, 320], P(None, 'batch'), may hold values from -0.3125 to 0.3125
- query_weight: bfloat16 [320, 320], P(None, 'batch'), may hold values from -30 to 30
- key_weight: bfloat16 [320, 320], P(None, 'batch'), may hold values from -1 to 1
- value_weight: bfloat16 [320, 320], P(None, 'batch'), may hold values from -0.625 to 0.625
- attn_out: bfloat16 [320, 320], P(None, 'batch'), may hold values from -0.625 to 0.625
- proj_outer: bfloat16 [320, 320], P(None, 'batch'), may hold values from -0.3125 to 0.3125
- outlet_conv: bfloat16 [2880, 4], replicated, may hold values from -0.109375 to 0.109375
- first_gain: float32 [320], replicated, may hold values from 0.1 to 1.9
- second_gain: float32 [320], replicated, may hold values from 0.1 to 1.9
- third_gain: float32 [320], replicated, may hold values from 0.1 to 1.9
- final_gain: float32 [320], replicated, may hold values from 0.1 to 1.9
- layer_gain: float32 [320], replicated, may hold values from 0.1 to 1.9
Outputs:
- guidance: float32 [64, 32, 64, 4], P('batch', 'space')
All inputs are finite; a program needn't handle non-finite values.
Results may differ from a plain program's by a relative error of at most 0.029.
Values may be sent and summed in bfloat16 or wider, within the bound.
A program may use at most 64 MiB of HBM per device.

v0:
```python
import math
import jax
import jax.numpy as jnp
from jax import lax
from jax.sharding import PartitionSpec as P

HEADS = 8
HEAD_SIZE = 40
GROUPS = 32
STEPS = 1000
EPS_GROUP = 1e-06
EPS_BLOCK = 1e-05
EPS_LAYER = 1e-05


def laid_out(parts, dim):
    parts = jnp.moveaxis(parts, 0, dim)
    shape = parts.shape
    return parts.reshape(*shape[:dim], shape[dim] * shape[dim + 1], *shape[dim + 2 :])


def from_everyone(shard, axis):
    length = lax.axis_size(axis)
    return lax.all_to_all(
        jnp.broadcast_to(shard[None], (length, *shard.shape)), axis, 0, 0, tiled=True
    )


def collect(shard, axis, dim):
    return laid_out(from_everyone(shard, axis), dim)


def extended(cells, sides, width):
    for axis, dim in sides:
        count = lax.axis_size(axis)
        ends = count - 1
        head = lax.slice_in_dim(cells, 0, width, axis=dim)
        tail = lax.slice_in_dim(cells, cells.shape[dim] - width, cells.shape[dim], axis=dim)
        cells = jnp.concatenate(
            [
                lax.ppermute(tail, axis, [(i, (i + 1) % count) for i in range(ends)]),
                cells,
                lax.ppermute(head, axis, [((i + 1) % count, i) for i in range(ends)]),
            ],
            axis=dim,
        )
    return cells


def of_everyone(shard, axis):
    everything = from_everyone(shard, axis)
    return jnp.sum(everything, axis=0)


def packed_total(arrays, axis):
    vector, at, gathered = (jnp.concatenate([a.reshape(-1) for a in arrays]), 0, [])
    running = of_everyone(vector, axis)
    for a in arrays:
        gathered.append(running[at : at + a.size].reshape(a.shape))
        at += a.size
    return tuple(gathered)


def in_one_piece(arrays, axis, dim, along):
    widths = [a.shape[along] for a in arrays]
    both = jnp.concatenate(arrays, axis=along)
    filled = lax.all_gather(both, axis, axis=dim, tiled=True)
    return tuple(jnp.split(filled, [sum(widths[:k]) for k in range(1, len(widths))], axis=along))


def turned_gather(arrays, axis, dims):
    turned = [jnp.moveaxis(a, dim, 0) for a, dim in zip(arrays, dims)]
    widths = [t[0].size for t in turned]
    both = jnp.concatenate([t.reshape(-1, w) for t, w in zip(turned, widths)], axis=1)
    filled = lax.all_gather(both, axis, axis=0, tiled=True)
    parts = jnp.split(filled, [sum(widths[:k]) for k in range(1, len(widths))], axis=1)
    return tuple(
        (
            jnp.moveaxis(b.reshape(-1, *t.shape[1:]), 0, dim)
            for b, t, dim in zip(parts, turned, dims)
        )
    )


def plan():
    fraction = jnp.arange(STEPS, dtype=jnp.float32) / (STEPS - 1)
    beta_root = math.sqrt(0.00085) + fraction * (math.sqrt(0.012) - math.sqrt(0.00085))
    return jnp.cumprod(1.0 - beta_root * beta_root)


def lookup(timesteps):
    plan_tab = plan()
    matches = jnp.arange(STEPS, dtype=jnp.int32)[None, :] == timesteps[:, None]
    return jnp.sum(jnp.where(matches, plan_tab[None, :], 0.0), axis=1)


def waveform_of(timesteps, halfway):
    frequency = jnp.exp(-math.log(10000.0) * jnp.arange(halfway, dtype=jnp.float32) / halfway)
    angles = timesteps.astype(jnp.float32)[:, None] * frequency[None, :]
    return jnp.concatenate([jnp.cos(angles), jnp.sin(angles)], axis=1).astype(jnp.bfloat16)


def embed_sharded(timesteps, first, first_bias, second, second_bias):
    all_steps = collect(timesteps, "batch", 0)
    position = lax.axis_index("batch")
    width_one = first.shape[1]
    width_two = second.shape[1]
    waveform = waveform_of(all_steps, first.shape[0] // 2)
    bias_one = lax.dynamic_slice_in_dim(first_bias, position * width_one, width_one, 0)
    inner = jax.nn.silu(jnp.dot(waveform, first, preferred_element_type=jnp.float32) + bias_one)
    hidden = jax.nn.silu(inner).astype(jnp.bfloat16)
    hidden_all = collect(hidden, "batch", 1)
    bias_two = lax.dynamic_slice_in_dim(second_bias, position * width_two, width_two, 0)
    columns = jnp.dot(hidden_all, second, preferred_element_type=jnp.float32) + bias_two
    return lax.all_to_all(columns, "batch", split_axis=0, concat_axis=1, tiled=True)


def convolve(padded, kernel):
    height = padded.shape[1] - 2
    breadth = padded.shape[2] - 2
    width_in = padded.shape[3]
    result = None
    for offset in range(9):
        row_off, col_off = (offset // 3, offset % 3)
        window = padded[:, row_off : row_off + height, col_off : col_off + breadth, :]
        partial_sum = jnp.einsum(
            "bhwc,cd->bhwd",
            window,
            kernel[offset * width_in : (offset + 1) * width_in],
            preferred_element_type=jnp.float32,
        )
        result = partial_sum if result is None else result + partial_sum
    return result


def with_rims(field):
    padded = extended(field, (("space", 1),), 1)
    return jnp.pad(padded, ((0, 0), (0, 0), (1, 1), (0, 0)))


def with_latent_rims(field):
    padded = extended(field, (("space", 1),), 1)
    return jnp.pad(padded, ((0, 0), (0, 0), (1, 1), (0, 0)))


def group_norm(field, gain_vec, epsilon):
    view_n, height, breadth, chan_n = field.shape
    grouped = field.reshape(view_n, height, breadth, GROUPS, chan_n // GROUPS)
    sums_local = jnp.sum(grouped, axis=(1, 2, 4))
    squares_local = jnp.sum(grouped * grouped, axis=(1, 2, 4))
    sums_all, squares_all = packed_total((sums_local, squares_local), "space")
    number = height * lax.axis_size("space") * breadth * (chan_n // GROUPS)
    means = sums_all / number
    squares = squares_all / number
    factor = lax.rsqrt(squares - means * means + epsilon)
    normal_f = (grouped - means[:, None, None, :, None]) * factor[:, None, None, :, None]
    return normal_f.reshape(view_n, height, breadth, chan_n) * gain_vec


def layer_norm(field, gain_vec):
    means = jnp.mean(field, axis=-1, keepdims=True)
    centred = field - means
    spread = jnp.mean(centred * centred, axis=-1, keepdims=True)
    return centred * lax.rsqrt(spread + EPS_LAYER) * gain_vec


def keys_everywhere(queries, key_rows, value_rows):
    view_n, token_n, chan_n = queries.shape
    factor = 1.0 / math.sqrt(HEAD_SIZE)
    query_heads = queries.reshape(view_n, token_n, HEADS, HEAD_SIZE)
    row_max = jnp.full((view_n, HEADS, token_n), -jnp.inf, jnp.float32)
    row_sum = jnp.zeros((view_n, HEADS, token_n), jnp.float32)
    accum = jnp.zeros((view_n, HEADS, token_n, HEAD_SIZE), jnp.float32)
    key_part, value_part = in_one_piece((key_rows, value_rows), "space", 1, 0)
    length = key_part.shape[1]
    block_n = min(512, length)
    for offset in range(0, length, block_n):
        key_blk = key_part[:, offset : offset + block_n]
        value_blk = value_part[:, offset : offset + block_n]
        rows_here = key_blk.shape[1]
        key_blk = key_blk.reshape(view_n, rows_here, HEADS, HEAD_SIZE)
        value_blk = value_blk.reshape(view_n, rows_here, HEADS, HEAD_SIZE)
        scores = (
            jnp.einsum("bqhd,bkhd->bhqk", query_heads, key_blk, preferred_element_type=jnp.float32)
            * factor
        )
        new_max = jnp.maximum(row_max, jnp.max(scores, axis=-1))
        shrink = jnp.exp(row_max - new_max)
        weights = jnp.exp(scores - new_max[..., None])
        row_sum = row_sum * shrink + jnp.sum(weights, axis=-1)
        accum = accum * shrink[..., None] + jnp.einsum(
            "bhqk,bkhd->bhqd",
            weights.astype(jnp.bfloat16),
            value_blk,
            preferred_element_type=jnp.float32,
        )
        row_max = new_max
    row_max, row_sum, accum = (row_max, row_sum, accum)
    result = accum / row_sum[..., None]
    return result.transpose(0, 2, 1, 3).reshape(view_n, token_n, chan_n).astype(jnp.bfloat16)


def project(field, matrix):
    return jnp.einsum("btc,cd->btd", field, matrix, preferred_element_type=jnp.float32)


def body(
    latents,
    noise_draw,
    timesteps,
    inlet_conv,
    time_first,
    time_first_bias,
    time_second,
    time_second_bias,
    conv_first,
    conv_second,
    proj_inner,
    query_weight,
    key_weight,
    value_weight,
    attn_out,
    proj_outer,
    outlet_conv,
    first_gain,
    second_gain,
    third_gain,
    final_gain,
    layer_gain,
):
    gathered = turned_gather(
        (
            conv_first,
            conv_second,
            proj_inner,
            query_weight,
            key_weight,
            value_weight,
            attn_out,
            proj_outer,
        ),
        "batch",
        (1, 1, 1, 1, 1, 1, 1, 1),
    )
    conv_one, conv_two, inner_w, query_w, key_w, value_w, output_w, outer_w = gathered
    embedded = embed_sharded(timesteps, time_first, time_first_bias, time_second, time_second_bias)
    alpha_bar = lookup(timesteps)[:, None, None, None]
    noisy = (jnp.sqrt(alpha_bar) * latents + jnp.sqrt(1.0 - alpha_bar) * noise_draw).astype(
        jnp.bfloat16
    )
    opening = convolve(with_latent_rims(noisy), inlet_conv).astype(jnp.bfloat16)
    active = jax.nn.silu(group_norm(opening.astype(jnp.float32), first_gain, EPS_BLOCK)).astype(
        jnp.bfloat16
    )
    middle = (convolve(with_rims(active), conv_one) + embedded[:, None, None, :]).astype(
        jnp.bfloat16
    )
    active = jax.nn.silu(group_norm(middle.astype(jnp.float32), second_gain, EPS_BLOCK)).astype(
        jnp.bfloat16
    )
    block_one = (opening.astype(jnp.float32) + convolve(with_rims(active), conv_two)).astype(
        jnp.bfloat16
    )
    normed = group_norm(block_one.astype(jnp.float32), third_gain, EPS_GROUP).astype(jnp.bfloat16)
    view_n, height, breadth, chan_n = normed.shape
    flattened = normed.reshape(view_n, height * breadth, chan_n)
    projected = project(flattened, inner_w)
    tokens_in = layer_norm(projected, layer_gain).astype(jnp.bfloat16)
    queries = project(tokens_in, query_w).astype(jnp.bfloat16)
    key_rows = project(tokens_in, key_w).astype(jnp.bfloat16)
    value_rows = project(tokens_in, value_w).astype(jnp.bfloat16)
    attended = keys_everywhere(queries, key_rows, value_rows)
    mixture = (project(attended, output_w) + projected).astype(jnp.bfloat16)
    outer = project(mixture, outer_w).reshape(view_n, height, breadth, chan_n)
    block_two = (block_one.astype(jnp.float32) + outer).astype(jnp.bfloat16)
    active = jax.nn.silu(group_norm(block_two.astype(jnp.float32), final_gain, EPS_BLOCK)).astype(
        jnp.bfloat16
    )
    predicted = convolve(with_rims(active), outlet_conv)
    return (1.0 - alpha_bar) * (predicted - noise_draw)


def solution(mesh):
    in_specs = (
        P("batch", "space", None, None),
        P("batch", "space", None, None),
        P("batch"),
        P(),
        P(None, "batch"),
        P(),
        P(None, "batch"),
        P(),
        P(None, "batch"),
        P(None, "batch"),
        P(None, "batch"),
        P(None, "batch"),
        P(None, "batch"),
        P(None, "batch"),
        P(None, "batch"),
        P(None, "batch"),
        P(),
        P(),
        P(),
        P(),
        P(),
        P(),
    )
    out_specs = P("batch", "space", None, None)
    return jax.shard_map(body, mesh=mesh, in_specs=in_specs, out_specs=out_specs, check_vma=False)
```

profile of v0, /device:TPU:1, one launch (start us, length us, event | category | flops | bytes accessed | tf_op | source)
XLA Modules:
  0.0 351.4 jit_solution(13570895085451096625)
XLA Ops:
  6.5 1.6 concatenate.63
  12.2 4.6 %collective-permute-start = (bf16[1,1,64,4]{2,3,1,0:T(4,128)(2,1)S(1)}, bf16[1,1,64,4]{2,3,1,0:T(4,128)(2,1)S(1)}, u32[]{:S(2)}, u32[]{:S(2)}) collective-permute-start(bf16[1,1,64,4]{2,3,1,0:T(4,128)(2,1)S(1)} %get-tuple-element.37), channel_id=1, source_target_pairs={{0,1},{1,2},{2,3},{3,4},{4,5},{5,6},{6,7},{8,9},{9,10},{10,11},{11... | collective-permute-start | bytes 1544 | tf_op jit(solution)/shard_map/ppermute | solution.py:41
  16.8 5.5 %collective-permute-start.1 = (bf16[1,1,64,4]{2,3,1,0:T(4,128)(2,1)S(1)}, bf16[1,1,64,4]{2,3,1,0:T(4,128)(2,1)S(1)}, u32[]{:S(2)}, u32[]{:S(2)}) collective-permute-start(bf16[1,1,64,4]{2,3,1,0:T(4,128)(2,1)S(1)} %get-tuple-element.38), channel_id=1, source_target_pairs={{1,0},{2,1},{3,2},{4,3},{5,4},{6,5},{7,6},{9,8},{10,9},{11,10},{12... | collective-permute-start | bytes 1544 | tf_op jit(solution)/shard_map/ppermute | solution.py:43
  22.8 14.3 %all-to-all-start.1 = ((s32[64,1,1]{2,1,0:T(1,128)}), s32[64,1,1]{2,1,0:T(1,128)S(1)}, u32[]{:S(2)}, u32[]{:S(2)}) async-start(s32[64,1,1]{2,1,0:T(1,128)} %broadcast_in_dim.22), calls=%async_computation.1 | async-start | bytes 65536 | tf_op jit(solution)/shard_map/all_to_all | solution.py:24
  38.7 11.6 %all-to-all-done.1 = s32[64,1,1]{2,1,0:T(1,128)S(1)} async-done(((s32[64,1,1]{2,1,0:T(1,128)}), s32[64,1,1]{2,1,0:T(1,128)S(1)}, u32[]{:S(2)}, u32[]{:S(2)}) %all-to-all-start.1) | async-done | bytes 288 | tf_op jit(solution)/shard_map/all_to_all | solution.py:24
  55.2 1.0 convolution_add_fusion.20
  60.2 5.1 %all-to-all-start = ((f32[8,1,64]{2,1,0:T(1,128)}), f32[8,1,64]{2,1,0:T(1,128)S(1)}, u32[]{:S(2)}, u32[]{:S(2)}) async-start(f32[8,1,64]{2,1,0:T(1,128)} %broadcast_in_dim.21), calls=%async_computation | async-start | bytes 8192 | tf_op jit(solution)/shard_map/all_to_all | solution.py:24
  66.2 3.9 %all-to-all-done = f32[8,1,64]{2,1,0:T(1,128)S(1)} async-done(((f32[8,1,64]{2,1,0:T(1,128)}), f32[8,1,64]{2,1,0:T(1,128)S(1)}, u32[]{:S(2)}, u32[]{:S(2)}) %all-to-all-start) | async-done | bytes 2080 | tf_op jit(solution)/shard_map/all_to_all | solution.py:24
  70.1 4.6 %all-to-all-start.2 = ((bf16[64,2,640]{2,1,0:T(2,128)(2,1)}), bf16[64,2,640]{2,1,0:T(2,128)(2,1)S(1)}, u32[]{:S(2)}, u32[]{:S(2)}) async-start(bf16[64,2,640]{2,1,0:T(2,128)(2,1)} %reshape.912), calls=%async_computation.2 | async-start | bytes 327680 | tf_op jit(solution)/shard_map/all_to_all | solution.py:24
  75.3 2.8 collective-permute-start.2
  78.1 1.9 collective-permute-start.3
  80.0 9.5 %all-to-all-done.2 = bf16[64,2,640]{2,1,0:T(2,128)(2,1)S(1)} async-done(((bf16[64,2,640]{2,1,0:T(2,128)(2,1)}), bf16[64,2,640]{2,1,0:T(2,128)(2,1)S(1)}, u32[]{:S(2)}, u32[]{:S(2)}) %all-to-all-start.2) | async-done | bytes 163872 | tf_op jit(solution)/shard_map/all_to_all | solution.py:24
  91.0 6.6 %all-to-all-start.3 = ((f32[64,1,5]{2,1,0:T(1,128)}), f32[64,1,5]{2,1,0:T(1,128)S(1)}, u32[]{:S(2)}, u32[]{:S(2)}) async-start(f32[64,1,5]{2,1,0:T(1,128)} %copy.45), calls=%async_computation.3 | async-start | bytes 65536 | tf_op jit(solution)/shard_map/all_to_all | solution.py:115
  97.8 12.9 %all-to-all-done.3 = f32[64,1,5]{2,1,0:T(1,128)S(1)} async-done(((f32[64,1,5]{2,1,0:T(1,128)}), f32[64,1,5]{2,1,0:T(1,128)S(1)}, u32[]{:S(2)}, u32[]{:S(2)}) %all-to-all-start.3) | async-done | bytes 1312 | tf_op jit(solution)/shard_map/all_to_all | solution.py:115
  112.1 89.3 %all-gather.6.cloned.1.call-done = bf16[64,5,7680]{2,1,0:T(8,128)(2,1)} async-done(((bf16[1,5,7680]{2,1,0:T(8,128)(2,1)}), bf16[64,5,7680]{2,1,0:T(8,128)(2,1)}) %all-gather.6.cloned.1.call-update) | async-done | bytes 4915216 | tf_op jit(solution)/shard_map/all_gather | solution.py:75
  201.4 8.5 %reshape.863 = bf16[320,7680]{1,0:T(8,128)(2,1)} reshape(bf16[64,5,7680]{2,1,0:T(8,128)(2,1)} %all-gather.6.cloned.1.call-done) | data formatting | bytes 9830400
  209.9 4.3 %fusion.187 = (bf16[320,2880]{1,0:T(8,128)(2,1)}, bf16[320,2880]{1,0:T(8,128)(2,1)S(1)}) fusion(bf16[320,7680]{1,0:T(8,128)(2,1)} %reshape.863), kind=kLoop, calls=%fused_computation.299 | loop fusion | bytes 7372800 | tf_op jit(solution)/shard_map/split | solution.py:76
  214.2 4.0 %copy.51 = bf16[320,2880]{0,1:T(8,128)(2,1)} copy(bf16[320,2880]{1,0:T(8,128)(2,1)} %get-tuple-element.20) | data formatting | bytes 3686400
  218.2 1.4 fusion.94
  219.5 1.2 fusion.95
  220.7 1.2 convolution_add_fusion.14
  222.0 1.2 convolution_add_fusion.13
  225.2 13.7 %all_to_all.48 = f32[8,1,64]{2,1,0:T(1,128)S(1)} all-to-all(f32[8,1,64]{2,1,0:T(1,128)S(1)} %broadcast_in_dim.24), channel_id=1, replica_groups=mesh['batch'=64,'space'=8] {'space'}, dimensions={0} | all-to-all | bytes 4096 | tf_op jit(solution)/shard_map/all_to_all | solution.py:24
  239.5 2.8 collective-permute-start.4
  242.3 2.1 collective-permute-start.5
  244.4 2.6 copy.52
  247.8 1.2 fusion.92
  249.0 1.2 fusion.93
  250.2 1.2 convolution_add_fusion.7
  251.4 1.2 convolution_add_fusion.6
  254.7 7.6 %all_to_all.49 = f32[8,1,64]{2,1,0:T(1,128)S(1)} all-to-all(f32[8,1,64]{2,1,0:T(1,128)S(1)} %broadcast_in_dim.26), channel_id=1, replica_groups=mesh['batch'=64,'space'=8] {'space'}, dimensions={0} | all-to-all | bytes 4096 | tf_op jit(solution)/shard_map/all_to_all | solution.py:24
  262.8 1.2 fusion.193
  264.2 1.2 fusion.59
  265.4 1.3 fusion.60
  267.4 1.3 convolution_convert_fusion.2
  268.7 38.4 %all-gather.4.cloned.1.call-done = bf16[2,2048,320]{1,2,0:T(8,128)(2,1)} async-done(((bf16[2,256,320]{1,2,0:T(8,128)(2,1)}), bf16[2,2048,320]{1,2,0:T(8,128)(2,1)}) %all-gather.4.cloned.1.call-update) | async-done | bytes 2621456 | tf_op jit(solution)/shard_map/all_gather | solution.py:67
  307.1 1.9 fusion.188
  312.3 2.2 fusion
  314.5 2.2 fusion.2
  316.7 1.2 fusion.32
  317.9 1.2 fusion.38
  319.2 1.2 fusion.44
  321.5 1.2 fusion.58
  322.8 1.3 fusion.182
  324.7 8.2 %all_to_all.50 = f32[8,1,64]{2,1,0:T(1,128)S(1)} all-to-all(f32[8,1,64]{2,1,0:T(1,128)S(1)} %broadcast_in_dim.28), channel_id=1, replica_groups=mesh['batch'=64,'space'=8] {'space'}, dimensions={0} | all-to-all | bytes 4096 | tf_op jit(solution)/shard_map/all_to_all | solution.py:24
  333.5 2.8 collective-permute-start.6
  336.3 1.9 collective-permute-start.7
  338.3 3.5 collective-permute-done.7
  (159 shorter events, 32.6 us)
Async XLA Ops:
  6.5 83.5 %copy-start = (bf16[1280,5]{0,1:T(8,128)(2,1)S(1)}, bf16[1280,5]{0,1:T(8,128)(2,1)}, u32[]{:S(2)}) copy-start(bf16[1280,5]{0,1:T(8,128)(2,1)} %param.28) | copy-start | bytes 38404
  6.5 51.6 %copy-start.3 = (bf16[36,320]{1,0:T(8,128)(2,1)S(1)}, bf16[36,320]{1,0:T(8,128)(2,1)}, u32[]{:S(2)}) copy-start(bf16[36,320]{1,0:T(8,128)(2,1)} %param.25) | copy-start | bytes 69124
  6.5 194.9 %all-gather.6.cloned.1.call-start = ((), (), s32[]{:S(2)}) async-start(), calls=%async_computation.8 | async-start | bytes 7987200 | tf_op jit(solution)/shard_map/all_gather | solution.py:75
  12.2 40.0 %collective-permute-start = (bf16[1,1,64,4]{2,3,1,0:T(4,128)(2,1)S(1)}, bf16[1,1,64,4]{2,3,1,0:T(4,128)(2,1)S(1)}, u32[]{:S(2)}, u32[]{:S(2)}) collective-permute-start(bf16[1,1,64,4]{2,3,1,0:T(4,128)(2,1)S(1)} %get-tuple-element.37), channel_id=1, source_target_pairs={{0,1},{1,2},{2,3},{3,4},{4,5},{5,6},{6,7},{8,9},{9,10},{10,11},{11... | collective-permute-start | bytes 1544 | tf_op jit(solution)/shard_map/ppermute | solution.py:41
  16.8 35.4 %collective-permute-start.1 = (bf16[1,1,64,4]{2,3,1,0:T(4,128)(2,1)S(1)}, bf16[1,1,64,4]{2,3,1,0:T(4,128)(2,1)S(1)}, u32[]{:S(2)}, u32[]{:S(2)}) collective-permute-start(bf16[1,1,64,4]{2,3,1,0:T(4,128)(2,1)S(1)} %get-tuple-element.38), channel_id=1, source_target_pairs={{1,0},{2,1},{3,2},{4,3},{5,4},{6,5},{7,6},{9,8},{10,9},{11,10},{12... | collective-permute-start | bytes 1544 | tf_op jit(solution)/shard_map/ppermute | solution.py:43
  22.8 27.5 %all-to-all-start.1 = ((s32[64,1,1]{2,1,0:T(1,128)}), s32[64,1,1]{2,1,0:T(1,128)S(1)}, u32[]{:S(2)}, u32[]{:S(2)}) async-start(s32[64,1,1]{2,1,0:T(1,128)} %broadcast_in_dim.22), calls=%async_computation.1 | async-start | bytes 65536 | tf_op jit(solution)/shard_map/all_to_all | solution.py:24
  51.2 24.0 %copy-start.5 = (f32[320]{0:T(512)S(1)}, f32[320]{0:T(512)}, u32[]{:S(2)}) copy-start(f32[320]{0:T(512)} %param.39) | copy-start | bytes 3844
  60.2 9.9 %all-to-all-start = ((f32[8,1,64]{2,1,0:T(1,128)}), f32[8,1,64]{2,1,0:T(1,128)S(1)}, u32[]{:S(2)}, u32[]{:S(2)}) async-start(f32[8,1,64]{2,1,0:T(1,128)} %broadcast_in_dim.21), calls=%async_computation | async-start | bytes 8192 | tf_op jit(solution)/shard_map/all_to_all | solution.py:24
  70.1 19.5 %all-to-all-start.2 = ((bf16[64,2,640]{2,1,0:T(2,128)(2,1)}), bf16[64,2,640]{2,1,0:T(2,128)(2,1)S(1)}, u32[]{:S(2)}, u32[]{:S(2)}) async-start(bf16[64,2,640]{2,1,0:T(2,128)(2,1)} %reshape.912), calls=%async_computation.2 | async-start | bytes 327680 | tf_op jit(solution)/shard_map/all_to_all | solution.py:24
  75.3 22.3 %collective-permute-start.2 = (bf16[1,1,64,320]{3,2,1,0:T(8,128)(2,1)S(1)}, bf16[1,1,64,320]{3,2,1,0:T(8,128)(2,1)S(1)}, u32[]{:S(2)}, u32[]{:S(2)}) collective-permute-start(bf16[1,1,64,320]{3,2,1,0:T(8,128)(2,1)S(1)} %get-tuple-element.34), channel_id=1, source_target_pairs={{0,1},{1,2},{2,3},{3,4},{4,5},{5,6},{6,7},{8,9},{9,10},{10,11},{11... | collective-permute-start | bytes 122888 | tf_op jit(solution)/shard_map/ppermute | solution.py:41
  78.1 19.6 %collective-permute-start.3 = (bf16[1,1,64,320]{3,2,1,0:T(8,128)(2,1)S(1)}, bf16[1,1,64,320]{3,2,1,0:T(8,128)(2,1)S(1)}, u32[]{:S(2)}, u32[]{:S(2)}) collective-permute-start(bf16[1,1,64,320]{3,2,1,0:T(8,128)(2,1)S(1)} %get-tuple-element.35), channel_id=1, source_target_pairs={{1,0},{2,1},{3,2},{4,3},{5,4},{6,5},{7,6},{9,8},{10,9},{11,10},{12... | collective-permute-start | bytes 122888 | tf_op jit(solution)/shard_map/ppermute | solution.py:43
  91.0 19.8 %all-to-all-start.3 = ((f32[64,1,5]{2,1,0:T(1,128)}), f32[64,1,5]{2,1,0:T(1,128)S(1)}, u32[]{:S(2)}, u32[]{:S(2)}) async-start(f32[64,1,5]{2,1,0:T(1,128)} %copy.45), calls=%async_computation.3 | async-start | bytes 65536 | tf_op jit(solution)/shard_map/all_to_all | solution.py:115
  97.6 209.5 %all-gather.4.cloned.1.call-start = ((), (), s32[]{:S(2)}) async-start(), calls=%async_computation.7 | async-start | bytes 2949120 | tf_op jit(solution)/shard_map/all_gather | solution.py:67
  218.2 5.0 %copy-start.2 = (bf16[320,2880]{0,1:T(8,128)(2,1)S(1)}, bf16[320,2880]{0,1:T(8,128)(2,1)}, u32[]{:S(2)}) copy-start(bf16[320,2880]{0,1:T(8,128)(2,1)} %copy.51) | copy-start | bytes 5529604
  223.2 16.1 %copy-start.6 = (f32[320]{0:T(512)S(1)}, f32[320]{0:T(512)}, u32[]{:S(2)}) copy-start(f32[320]{0:T(512)} %param.40) | copy-start | bytes 3844
  239.5 7.5 %collective-permute-start.4 = (bf16[1,1,64,320]{3,2,1,0:T(8,128)(2,1)S(1)}, bf16[1,1,64,320]{3,2,1,0:T(8,128)(2,1)S(1)}, u32[]{:S(2)}, u32[]{:S(2)}) collective-permute-start(bf16[1,1,64,320]{3,2,1,0:T(8,128)(2,1)S(1)} %get-tuple-element.32), channel_id=1, source_target_pairs={{0,1},{1,2},{2,3},{3,4},{4,5},{5,6},{6,7},{8,9},{9,10},{10,11},{11... | collective-permute-start | bytes 122888 | tf_op jit(solution)/shard_map/ppermute | solution.py:41
  242.3 5.4 %collective-permute-start.5 = (bf16[1,1,64,320]{3,2,1,0:T(8,128)(2,1)S(1)}, bf16[1,1,64,320]{3,2,1,0:T(8,128)(2,1)S(1)}, u32[]{:S(2)}, u32[]{:S(2)}) collective-permute-start(bf16[1,1,64,320]{3,2,1,0:T(8,128)(2,1)S(1)} %get-tuple-element.33), channel_id=1, source_target_pairs={{1,0},{2,1},{3,2},{4,3},{5,4},{6,5},{7,6},{9,8},{10,9},{11,10},{12... | collective-permute-start | bytes 122888 | tf_op jit(solution)/shard_map/ppermute | solution.py:43
  247.0 5.6 %copy-start.1 = (bf16[320,2880]{0,1:T(8,128)(2,1)S(1)}, bf16[320,2880]{0,1:T(8,128)(2,1)}, u32[]{:S(2)}) copy-start(bf16[320,2880]{0,1:T(8,128)(2,1)} %copy.52) | copy-start | bytes 5529604
  252.6 10.0 %copy-start.7 = (f32[320]{0:T(512)S(1)}, f32[320]{0:T(512)}, u32[]{:S(2)}) copy-start(f32[320]{0:T(512)} %param.41) | copy-start | bytes 3844
  252.9 11.2 %copy-start.8 = (f32[320]{0:T(512)S(1)}, f32[320]{0:T(512)}, u32[]{:S(2)}) copy-start(f32[320]{0:T(512)} %param.43) | copy-start | bytes 3844
  320.4 13.0 %copy-start.9 = (f32[320]{0:T(512)S(1)}, f32[320]{0:T(512)}, u32[]{:S(2)}) copy-start(f32[320]{0:T(512)} %param.42) | copy-start | bytes 3844
  320.4 21.4 %copy-start.10 = (bf16[2880,4]{0,1:T(4,128)(2,1)S(1)}, bf16[2880,4]{0,1:T(4,128)(2,1)}, u32[]{:S(2)}) copy-start(bf16[2880,4]{0,1:T(4,128)(2,1)} %param.38) | copy-start | bytes 69124
  321.4 22.2 %copy-start.4 = (f32[1,4,64,4]{2,3,1,0:T(4,128)S(1)}, f32[1,4,64,4]{2,3,1,0:T(4,128)}, u32[]{:S(2)}) copy-start(f32[1,4,64,4]{2,3,1,0:T(4,128)} %param.23) | copy-start | bytes 12292
  333.5 4.7 %collective-permute-start.6 = (bf16[1,1,64,320]{3,2,1,0:T(8,128)(2,1)S(1)}, bf16[1,1,64,320]{3,2,1,0:T(8,128)(2,1)S(1)}, u32[]{:S(2)}, u32[]{:S(2)}) collective-permute-start(bf16[1,1,64,320]{3,2,1,0:T(8,128)(2,1)S(1)} %get-tuple-element.30), channel_id=1, source_target_pairs={{0,1},{1,2},{2,3},{3,4},{4,5},{5,6},{6,7},{8,9},{9,10},{10,11},{11... | collective-permute-start | bytes 122888 | tf_op jit(solution)/shard_map/ppermute | solution.py:41
  336.3 5.4 %collective-permute-start.7 = (bf16[1,1,64,320]{3,2,1,0:T(8,128)(2,1)S(1)}, bf16[1,1,64,320]{3,2,1,0:T(8,128)(2,1)S(1)}, u32[]{:S(2)}, u32[]{:S(2)}) collective-permute-start(bf16[1,1,64,320]{3,2,1,0:T(8,128)(2,1)S(1)} %get-tuple-element.31), channel_id=1, source_target_pairs={{1,0},{2,1},{3,2},{4,3},{5,4},{6,5},{7,6},{9,8},{10,9},{11,10},{12... | collective-permute-start | bytes 122888 | tf_op jit(solution)/shard_map/ppermute | solution.py:43
Sparse Core Ops, SparseCore 0:
  11.9 189.5 all-gather.5
  267.6 39.4 all-gather.3
where the time goes:
time: 353 us; the launch traced here: 351 us
  waiting for transfers between devices  170 us (48%)
  starting transfers between devices  55 us (16%)
  matrix products  38.7 us (11%)
  local copies, waits for them, and re-layouts  31.1 us (9%)
  blocking collectives  29.4 us (8%)
  between operations  16.2 us (5%)
  other arithmetic  11.2 us (3%)
    all_gather x1, waiting for transfers between devices, turned_gather(): filled = lax.all_gather(both, axis, axis=0, tiled=True)  89.3 us
    all_gather x1, waiting for transfers between devices, in_one_piece(): filled = lax.all_gather(both, axis, axis=dim, tiled=True)  38.4 us
    all_to_all x3, blocking collectives, from_everyone(): lax.all_to_all(jnp.broadcast_to(shard[None], (length, *shard.shape)), axi...  29.4 us
    all_to_all x3, waiting for transfers between devices, from_everyone(): lax.all_to_all(jnp.broadcast_to(shard[None], (length, *shard.shape)), axi...  25 us
    all_to_all x3, starting transfers between devices, from_everyone(): lax.all_to_all(jnp.broadcast_to(shard[None], (length, *shard.shape)), axi...  24 us
    dot_general x36, matrix products, convolve(): jnp.einsum('bhwc,cd->bhwd', window, kernel[offset * width_in:(offset + 1)...  22.1 us
    unnamed x28, local copies, waits for them, and re-layouts  16.4 us
    ppermute x4, starting transfers between devices, extended(): lax.ppermute(tail, axis, [(i, (i + 1) % count) for i in range(ends)])  12.9 us
  transfers between devices with their start and end apart: 14, of which 8 were waited for; matrix products, arithmetic and copies ran while one was open for 6% of the time, Pallas kernels for 0%

commit v1 on v0

--- a/solution.py
+++ b/solution.py
@@ -72,7 +72,9 @@
     turned = [jnp.moveaxis(a, dim, 0) for a, dim in zip(arrays, dims)]
     widths = [t[0].size for t in turned]
     both = jnp.concatenate([t.reshape(-1, w) for t, w in zip(turned, widths)], axis=1)
-    filled = lax.all_gather(both, axis, axis=0, tiled=True)
+    filled = jnp.concatenate(
+        lax.all_to_all(jnp.stack([both] * lax.axis_size(axis)), axis, 0, 0), axis=0
+    )
     parts = jnp.split(filled, [sum(widths[:k]) for k in range(1, len(widths))], axis=1)
     return tuple(
         (

time: 353 us -> 474 us (1.34)
  waiting for transfers between devices: 170 us -> 275 us
  starting transfers between devices: 55 us -> 63.4 us
  blocking collectives: 29.4 us -> 35.2 us
    ppermute x4, waiting for transfers between devices: 0.01 us -> 177 us  [extended(): lax.ppermute(tail, axis, [(i, (i + 1) % count) for i in range(ends)])]
    all_gather x1 -> x0, waiting for transfers between devices: 89.3 us -> none  [turned_gather(): filled = lax.all_gather(both, axis, axis=0, tiled=True)]
    ppermute x4, waiting for transfers between devices: 4.15 us -> 23.5 us  [extended(): lax.ppermute(head, axis, [((i + 1) % count, i) for i in range(ends)])]
    reshape x1 -> x2, local copies, waits for them, and re-layouts: 0.01 us -> 8.47 us  [the longest x1 8.47 us: turned_gather(): jnp.concatenate(lax.all_to_all(jnp.stack([both] * lax.axis_size(axis)), a...]
    unnamed x28 -> x45, local copies, waits for them, and re-layouts: 16.4 us -> 7.98 us
    all_to_all x0 -> x1, starting transfers between devices: none -> 5.84 us  [turned_gather(): lax.all_to_all(jnp.stack([both] * lax.axis_size(axis)), axis, 0, 0)]
    all_to_all x3, blocking collectives: 29.4 us -> 35.2 us  [from_everyone(): lax.all_to_all(jnp.broadcast_to(shard[None], (length, *shard.shape)), axi...]
  transfers between devices with their start and end apart: 14 -> 14, of which waited for: 8 -> 9; matrix products, arithmetic and copies ran while one was open for 6% -> 4% of each run, Pallas kernels for 0% -> 0%
where the time goes in v1:
time: 474 us; the launch traced here: 472 us
  waiting for transfers between devices  275 us (58%)
  starting transfers between devices  63.4 us (13%)
  matrix products  37.3 us (8%)
  blocking collectives  35.2 us (7%)
  local copies, waits for them, and re-layouts  33.3 us (7%)
  between operations  16.5 us (3%)
  other arithmetic  11.2 us (2%)
    ppermute x4, waiting for transfers between devices, extended(): lax.ppermute(tail, axis, [(i, (i + 1) % count) for i in range(ends)])  177 us
    all_gather x1, waiting for transfers between devices, in_one_piece(): filled = lax.all_gather(both, axis, axis=dim, tiled=True)  39.1 us
    all_to_all x3, blocking collectives, from_everyone(): lax.all_to_all(jnp.broadcast_to(shard[None], (length, *shard.shape)), axi...  35.2 us
    all_to_all x3, starting transfers between devices, from_everyone(): lax.all_to_all(jnp.broadcast_to(shard[None], (length, *shard.shape)), axi...  25.3 us
    ppermute x4, waiting for transfers between devices, extended(): lax.ppermute(head, axis, [((i + 1) % count, i) for i in range(ends)])  23.5 us
    all_to_all x3, waiting for transfers between devices, from_everyone(): lax.all_to_all(jnp.broadcast_to(shard[None], (length, *shard.shape)), axi...  22.2 us
    dot_general x36, matrix products, convolve(): jnp.einsum('bhwc,cd->bhwd', window, kernel[offset * width_in:(offset + 1)...  20.7 us
    ppermute x4, starting transfers between devices, extended(): lax.ppermute(tail, axis, [(i, (i + 1) % count) for i in range(ends)])  14.4 us
  transfers between devices with their start and end apart: 14, of which 9 were waited for; matrix products, arithmetic and copies ran while one was open for 4% of the time, Pallas kernels for 0%

profile of v1, /device:TPU:1, one launch (start us, length us, event | category | flops | bytes accessed | tf_op | source)
XLA Modules:
  0.0 471.9 jit_solution(3378530029774866280)
XLA Ops:
  10.7 4.6 collective-permute-start
  15.3 5.5 %collective-permute-start.1 = (bf16[1,1,64,4]{2,3,1,0:T(4,128)(2,1)S(1)}, bf16[1,1,64,4]{2,3,1,0:T(4,128)(2,1)S(1)}, u32[]{:S(2)}, u32[]{:S(2)}) collective-permute-start(bf16[1,1,64,4]{2,3,1,0:T(4,128)(2,1)S(1)} %get-tuple-element.38), channel_id=1, source_target_pairs={{1,0},{2,1},{3,2},{4,3},{5,4},{6,5},{7,6},{9,8},{10,9},{11,10},{12... | collective-permute-start | bytes 1544 | tf_op jit(solution)/shard_map/ppermute | solution.py:43
  21.4 14.3 %all-to-all-start.2 = ((s32[64,1,1]{2,1,0:T(1,128)}), s32[64,1,1]{2,1,0:T(1,128)S(1)}, u32[]{:S(2)}, u32[]{:S(2)}) async-start(s32[64,1,1]{2,1,0:T(1,128)} %broadcast_in_dim.22), calls=%async_computation.2 | async-start | bytes 65536 | tf_op jit(solution)/shard_map/all_to_all | solution.py:24
  37.2 11.6 %all-to-all-done.2 = s32[64,1,1]{2,1,0:T(1,128)S(1)} async-done(((s32[64,1,1]{2,1,0:T(1,128)}), s32[64,1,1]{2,1,0:T(1,128)S(1)}, u32[]{:S(2)}, u32[]{:S(2)}) %all-to-all-start.2) | async-done | bytes 288 | tf_op jit(solution)/shard_map/all_to_all | solution.py:24
  51.6 4.6 all-to-all-start.3
  62.4 7.2 %all-to-all-done.3 = bf16[64,2,640]{2,1,0:T(2,128)(2,1)S(1)} async-done(((bf16[64,2,640]{2,1,0:T(2,128)(2,1)}), bf16[64,2,640]{2,1,0:T(2,128)(2,1)S(1)}, u32[]{:S(2)}, u32[]{:S(2)}) %all-to-all-start.3) | async-done | bytes 163872 | tf_op jit(solution)/shard_map/all_to_all | solution.py:24
  70.2 6.3 %all-to-all-start = ((f32[8,1,64]{2,1,0:T(1,128)}), f32[8,1,64]{2,1,0:T(1,128)S(1)}, u32[]{:S(2)}, u32[]{:S(2)}) async-start(f32[8,1,64]{2,1,0:T(1,128)} %broadcast_in_dim.21), calls=%async_computation | async-start | bytes 8192 | tf_op jit(solution)/shard_map/all_to_all | solution.py:24
  77.9 3.4 all-to-all-done
  81.3 6.4 %all-to-all-start.4 = ((f32[64,1,5]{2,1,0:T(1,128)}), f32[64,1,5]{2,1,0:T(1,128)S(1)}, u32[]{:S(2)}, u32[]{:S(2)}) async-start(f32[64,1,5]{2,1,0:T(1,128)} %copy.45), calls=%async_computation.4 | async-start | bytes 65536 | tf_op jit(solution)/shard_map/all_to_all | solution.py:117
  88.0 12.9 %all-to-all-done.4 = f32[64,1,5]{2,1,0:T(1,128)S(1)} async-done(((f32[64,1,5]{2,1,0:T(1,128)}), f32[64,1,5]{2,1,0:T(1,128)S(1)}, u32[]{:S(2)}, u32[]{:S(2)}) %all-to-all-start.4) | async-done | bytes 1312 | tf_op jit(solution)/shard_map/all_to_all | solution.py:117
  100.9 3.7 stack.2
  104.6 5.8 %all-to-all-start.1 = ((bf16[64,5,7680]{2,1,0:T(8,128)(2,1)}), bf16[64,5,7680]{2,1,0:T(8,128)(2,1)}, u32[]{:S(2)}, u32[]{:S(2)}) async-start(bf16[64,5,7680]{2,1,0:T(8,128)(2,1)} %stack.2), calls=%async_computation.1 | async-start | bytes 15728640 | tf_op jit(solution)/shard_map/all_to_all | solution.py:76
  111.1 4.3 collective-permute-start.2
  115.4 2.1 collective-permute-start.3
  117.5 177.2 %collective-permute-done.2 = bf16[1,1,64,320]{3,2,1,0:T(8,128)(2,1)S(1)} collective-permute-done((bf16[1,1,64,320]{3,2,1,0:T(8,128)(2,1)S(1)}, bf16[1,1,64,320]{3,2,1,0:T(8,128)(2,1)S(1)}, u32[]{:S(2)}, u32[]{:S(2)}) %collective-permute-start.2) | collective-permute-done | bytes 40992 | tf_op jit(solution)/shard_map/ppermute | solution.py:41
  294.7 19.2 %collective-permute-done.3 = bf16[1,1,64,320]{3,2,1,0:T(8,128)(2,1)S(1)} collective-permute-done((bf16[1,1,64,320]{3,2,1,0:T(8,128)(2,1)S(1)}, bf16[1,1,64,320]{3,2,1,0:T(8,128)(2,1)S(1)}, u32[]{:S(2)}, u32[]{:S(2)}) %collective-permute-start.3) | collective-permute-done | bytes 40992 | tf_op jit(solution)/shard_map/ppermute | solution.py:43
  315.4 8.5 %reshape.834 = bf16[320,7680]{1,0:T(8,128)(2,1)} reshape(bf16[64,5,7680]{2,1,0:T(8,128)(2,1)} %all-to-all-done.1) | data formatting | bytes 9830400 | tf_op jit(solution)/shard_map/reshape | solution.py:75
  323.9 4.3 fusion.187
  328.2 4.0 copy.51
  332.1 1.4 fusion.94
  333.5 1.2 fusion.95
  334.7 1.2 convolution_add_fusion.14
  335.9 1.2 convolution_add_fusion.13
  339.1 19.6 %all_to_all.53 = f32[8,1,64]{2,1,0:T(1,128)S(1)} all-to-all(f32[8,1,64]{2,1,0:T(1,128)S(1)} %broadcast_in_dim.24), channel_id=1, replica_groups=mesh['batch'=64,'space'=8] {'space'}, dimensions={0} | all-to-all | bytes 4096 | tf_op jit(solution)/shard_map/all_to_all | solution.py:24
  359.4 2.8 collective-permute-start.4
  362.2 1.9 collective-permute-start.5
  364.1 2.6 copy.52
  367.7 1.2 fusion.92
  368.9 1.2 fusion.93
  370.1 1.2 convolution_add_fusion.7
  371.3 1.2 convolution_add_fusion.6
  374.6 7.4 %all_to_all.54 = f32[8,1,64]{2,1,0:T(1,128)S(1)} all-to-all(f32[8,1,64]{2,1,0:T(1,128)S(1)} %broadcast_in_dim.26), channel_id=1, replica_groups=mesh['batch'=64,'space'=8] {'space'}, dimensions={0} | all-to-all | bytes 4096 | tf_op jit(solution)/shard_map/all_to_all | solution.py:24
  382.5 1.2 fusion.193
  385.1 1.3 fusion.60
  387.2 1.3 convolution_convert_fusion.2
  388.4 39.1 %all-gather.2.cloned.1.call-done = bf16[2,2048,320]{1,2,0:T(8,128)(2,1)} async-done(((bf16[2,256,320]{1,2,0:T(8,128)(2,1)}), bf16[2,2048,320]{1,2,0:T(8,128)(2,1)}) %all-gather.2.cloned.1.call-update) | async-done | bytes 2621456 | tf_op jit(solution)/shard_map/all_gather | solution.py:67
  427.6 1.9 fusion.188
  432.8 2.2 fusion
  435.0 2.2 fusion.2
  437.2 1.2 fusion.32
  438.4 1.2 fusion.38
  439.6 1.2 fusion.44
  441.9 1.2 fusion.58
  443.3 1.3 fusion.182
  445.2 8.2 %all_to_all.55 = f32[8,1,64]{2,1,0:T(1,128)S(1)} all-to-all(f32[8,1,64]{2,1,0:T(1,128)S(1)} %broadcast_in_dim.28), channel_id=1, replica_groups=mesh['batch'=64,'space'=8] {'space'}, dimensions={0} | all-to-all | bytes 4096 | tf_op jit(solution)/shard_map/all_to_all | solution.py:24
  454.0 2.8 collective-permute-start.6
  456.8 1.9 collective-permute-start.7
  458.8 3.5 collective-permute-done.7
  (177 shorter events, 33.8 us)
Async XLA Ops:
  6.5 70.5 %copy-start = (bf16[1280,5]{0,1:T(8,128)(2,1)S(1)}, bf16[1280,5]{0,1:T(8,128)(2,1)}, u32[]{:S(2)}) copy-start(bf16[1280,5]{0,1:T(8,128)(2,1)} %param.28) | copy-start | bytes 38404
  6.5 53.9 %copy-start.4 = (bf16[36,320]{1,0:T(8,128)(2,1)S(1)}, bf16[36,320]{1,0:T(8,128)(2,1)}, u32[]{:S(2)}) copy-start(bf16[36,320]{1,0:T(8,128)(2,1)} %param.25) | copy-start | bytes 69124
  10.7 45.6 %collective-permute-start = (bf16[1,1,64,4]{2,3,1,0:T(4,128)(2,1)S(1)}, bf16[1,1,64,4]{2,3,1,0:T(4,128)(2,1)S(1)}, u32[]{:S(2)}, u32[]{:S(2)}) collective-permute-start(bf16[1,1,64,4]{2,3,1,0:T(4,128)(2,1)S(1)} %get-tuple-element.37), channel_id=1, source_target_pairs={{0,1},{1,2},{2,3},{3,4},{4,5},{5,6},{6,7},{8,9},{9,10},{10,11},{11... | collective-permute-start | bytes 1544 | tf_op jit(solution)/shard_map/ppermute | solution.py:41
  15.3 41.0 %collective-permute-start.1 = (bf16[1,1,64,4]{2,3,1,0:T(4,128)(2,1)S(1)}, bf16[1,1,64,4]{2,3,1,0:T(4,128)(2,1)S(1)}, u32[]{:S(2)}, u32[]{:S(2)}) collective-permute-start(bf16[1,1,64,4]{2,3,1,0:T(4,128)(2,1)S(1)} %get-tuple-element.38), channel_id=1, source_target_pairs={{1,0},{2,1},{3,2},{4,3},{5,4},{6,5},{7,6},{9,8},{10,9},{11,10},{12... | collective-permute-start | bytes 1544 | tf_op jit(solution)/shard_map/ppermute | solution.py:43
  21.4 27.5 %all-to-all-start.2 = ((s32[64,1,1]{2,1,0:T(1,128)}), s32[64,1,1]{2,1,0:T(1,128)S(1)}, u32[]{:S(2)}, u32[]{:S(2)}) async-start(s32[64,1,1]{2,1,0:T(1,128)} %broadcast_in_dim.22), calls=%async_computation.2 | async-start | bytes 65536 | tf_op jit(solution)/shard_map/all_to_all | solution.py:24
  51.6 18.0 %all-to-all-start.3 = ((bf16[64,2,640]{2,1,0:T(2,128)(2,1)}), bf16[64,2,640]{2,1,0:T(2,128)(2,1)S(1)}, u32[]{:S(2)}, u32[]{:S(2)}) async-start(bf16[64,2,640]{2,1,0:T(2,128)(2,1)} %reshape.916), calls=%async_computation.3 | async-start | bytes 327680 | tf_op jit(solution)/shard_map/all_to_all | solution.py:24
  58.3 29.4 %copy-start.5 = (bf16[2880,5]{0,1:T(8,128)(2,1)S(1)}, bf16[2880,5]{0,1:T(8,128)(2,1)}, u32[]{:S(2)}) copy-start(bf16[2880,5]{0,1:T(8,128)(2,1)} %param.30) | copy-start | bytes 86404
  58.3 29.4 %copy-start.6 = (bf16[2880,5]{0,1:T(8,128)(2,1)S(1)}, bf16[2880,5]{0,1:T(8,128)(2,1)}, u32[]{:S(2)}) copy-start(bf16[2880,5]{0,1:T(8,128)(2,1)} %param.31) | copy-start | bytes 86404
  58.4 29.4 %copy-start.8 = (bf16[320,5]{0,1:T(8,128)(2,1)S(1)}, bf16[320,5]{0,1:T(8,128)(2,1)}, u32[]{:S(2)}) copy-start(bf16[320,5]{0,1:T(8,128)(2,1)} %param.32) | copy-start | bytes 9604
  58.4 29.4 %copy-start.9 = (bf16[320,5]{0,1:T(8,128)(2,1)S(1)}, bf16[320,5]{0,1:T(8,128)(2,1)}, u32[]{:S(2)}) copy-start(bf16[320,5]{0,1:T(8,128)(2,1)} %param.33) | copy-start | bytes 9604
  58.4 29.4 %copy-start.10 = (bf16[320,5]{0,1:T(8,128)(2,1)S(1)}, bf16[320,5]{0,1:T(8,128)(2,1)}, u32[]{:S(2)}) copy-start(bf16[320,5]{0,1:T(8,128)(2,1)} %param.34) | copy-start | bytes 9604
  58.4 29.4 %copy-start.11 = (bf16[320,5]{0,1:T(8,128)(2,1)S(1)}, bf16[320,5]{0,1:T(8,128)(2,1)}, u32[]{:S(2)}) copy-start(bf16[320,5]{0,1:T(8,128)(2,1)} %param.35) | copy-start | bytes 9604
  58.4 29.4 %copy-start.12 = (bf16[320,5]{0,1:T(8,128)(2,1)S(1)}, bf16[320,5]{0,1:T(8,128)(2,1)}, u32[]{:S(2)}) copy-start(bf16[320,5]{0,1:T(8,128)(2,1)} %param.36) | copy-start | bytes 9604
  58.4 29.4 %copy-start.13 = (bf16[320,5]{0,1:T(8,128)(2,1)S(1)}, bf16[320,5]{0,1:T(8,128)(2,1)}, u32[]{:S(2)}) copy-start(bf16[320,5]{0,1:T(8,128)(2,1)} %param.37) | copy-start | bytes 9604
  70.2 11.1 %all-to-all-start = ((f32[8,1,64]{2,1,0:T(1,128)}), f32[8,1,64]{2,1,0:T(1,128)S(1)}, u32[]{:S(2)}, u32[]{:S(2)}) async-start(f32[8,1,64]{2,1,0:T(1,128)} %broadcast_in_dim.21), calls=%async_computation | async-start | bytes 8192 | tf_op jit(solution)/shard_map/all_to_all | solution.py:24
  81.3 19.6 %all-to-all-start.4 = ((f32[64,1,5]{2,1,0:T(1,128)}), f32[64,1,5]{2,1,0:T(1,128)S(1)}, u32[]{:S(2)}, u32[]{:S(2)}) async-start(f32[64,1,5]{2,1,0:T(1,128)} %copy.45), calls=%async_computation.4 | async-start | bytes 65536 | tf_op jit(solution)/shard_map/all_to_all | solution.py:117
  104.6 6.4 %copy-start.14 = (f32[320]{0:T(512)S(1)}, f32[320]{0:T(512)}, u32[]{:S(2)}) copy-start(f32[320]{0:T(512)} %param.39) | copy-start | bytes 3844
  104.6 210.8 %all-to-all-start.1 = ((bf16[64,5,7680]{2,1,0:T(8,128)(2,1)}), bf16[64,5,7680]{2,1,0:T(8,128)(2,1)}, u32[]{:S(2)}, u32[]{:S(2)}) async-start(bf16[64,5,7680]{2,1,0:T(8,128)(2,1)} %stack.2), calls=%async_computation.1 | async-start | bytes 15728640 | tf_op jit(solution)/shard_map/all_to_all | solution.py:76
  110.4 317.1 %all-gather.2.cloned.1.call-start = ((), (), s32[]{:S(2)}) async-start(), calls=%async_computation.8 | async-start | bytes 2949120 | tf_op jit(solution)/shard_map/all_gather | solution.py:67
  111.1 183.6 %collective-permute-start.2 = (bf16[1,1,64,320]{3,2,1,0:T(8,128)(2,1)S(1)}, bf16[1,1,64,320]{3,2,1,0:T(8,128)(2,1)S(1)}, u32[]{:S(2)}, u32[]{:S(2)}) collective-permute-start(bf16[1,1,64,320]{3,2,1,0:T(8,128)(2,1)S(1)} %get-tuple-element.34), channel_id=1, source_target_pairs={{0,1},{1,2},{2,3},{3,4},{4,5},{5,6},{6,7},{8,9},{9,10},{10,11},{11... | collective-permute-start | bytes 122888 | tf_op jit(solution)/shard_map/ppermute | solution.py:41
  115.4 198.5 %collective-permute-start.3 = (bf16[1,1,64,320]{3,2,1,0:T(8,128)(2,1)S(1)}, bf16[1,1,64,320]{3,2,1,0:T(8,128)(2,1)S(1)}, u32[]{:S(2)}, u32[]{:S(2)}) collective-permute-start(bf16[1,1,64,320]{3,2,1,0:T(8,128)(2,1)S(1)} %get-tuple-element.35), channel_id=1, source_target_pairs={{1,0},{2,1},{3,2},{4,3},{5,4},{6,5},{7,6},{9,8},{10,9},{11,10},{12... | collective-permute-start | bytes 122888 | tf_op jit(solution)/shard_map/ppermute | solution.py:43
  332.1 5.0 %copy-start.3 = (bf16[320,2880]{0,1:T(8,128)(2,1)S(1)}, bf16[320,2880]{0,1:T(8,128)(2,1)}, u32[]{:S(2)}) copy-start(bf16[320,2880]{0,1:T(8,128)(2,1)} %copy.51) | copy-start | bytes 5529604
  337.2 22.0 %copy-start.15 = (f32[320]{0:T(512)S(1)}, f32[320]{0:T(512)}, u32[]{:S(2)}) copy-start(f32[320]{0:T(512)} %param.40) | copy-start | bytes 3844
  359.4 7.3 %collective-permute-start.4 = (bf16[1,1,64,320]{3,2,1,0:T(8,128)(2,1)S(1)}, bf16[1,1,64,320]{3,2,1,0:T(8,128)(2,1)S(1)}, u32[]{:S(2)}, u32[]{:S(2)}) collective-permute-start(bf16[1,1,64,320]{3,2,1,0:T(8,128)(2,1)S(1)} %get-tuple-element.32), channel_id=1, source_target_pairs={{0,1},{1,2},{2,3},{3,4},{4,5},{5,6},{6,7},{8,9},{9,10},{10,11},{11... | collective-permute-start | bytes 122888 | tf_op jit(solution)/shard_map/ppermute | solution.py:41
  362.2 5.4 %collective-permute-start.5 = (bf16[1,1,64,320]{3,2,1,0:T(8,128)(2,1)S(1)}, bf16[1,1,64,320]{3,2,1,0:T(8,128)(2,1)S(1)}, u32[]{:S(2)}, u32[]{:S(2)}) collective-permute-start(bf16[1,1,64,320]{3,2,1,0:T(8,128)(2,1)S(1)} %get-tuple-element.33), channel_id=1, source_target_pairs={{1,0},{2,1},{3,2},{4,3},{5,4},{6,5},{7,6},{9,8},{10,9},{11,10},{12... | collective-permute-start | bytes 122888 | tf_op jit(solution)/shard_map/ppermute | solution.py:43
  366.7 5.8 %copy-start.2 = (bf16[320,2880]{0,1:T(8,128)(2,1)S(1)}, bf16[320,2880]{0,1:T(8,128)(2,1)}, u32[]{:S(2)}) copy-start(bf16[320,2880]{0,1:T(8,128)(2,1)} %copy.52) | copy-start | bytes 5529604
  372.5 9.8 %copy-start.16 = (f32[320]{0:T(512)S(1)}, f32[320]{0:T(512)}, u32[]{:S(2)}) copy-start(f32[320]{0:T(512)} %param.41) | copy-start | bytes 3844
  372.8 11.0 %copy-start.17 = (f32[320]{0:T(512)S(1)}, f32[320]{0:T(512)}, u32[]{:S(2)}) copy-start(f32[320]{0:T(512)} %param.43) | copy-start | bytes 3844
  440.9 13.0 %copy-start.18 = (f32[320]{0:T(512)S(1)}, f32[320]{0:T(512)}, u32[]{:S(2)}) copy-start(f32[320]{0:T(512)} %param.42) | copy-start | bytes 3844
  440.9 21.4 %copy-start.19 = (bf16[2880,4]{0,1:T(4,128)(2,1)S(1)}, bf16[2880,4]{0,1:T(4,128)(2,1)}, u32[]{:S(2)}) copy-start(bf16[2880,4]{0,1:T(4,128)(2,1)} %param.38) | copy-start | bytes 69124
  441.9 22.3 %copy-start.7 = (f32[1,4,64,4]{2,3,1,0:T(4,128)S(1)}, f32[1,4,64,4]{2,3,1,0:T(4,128)}, u32[]{:S(2)}) copy-start(f32[1,4,64,4]{2,3,1,0:T(4,128)} %param.23) | copy-start | bytes 12292
  441.9 23.1 %copy-start.1 = (bf16[1280,5]{0,1:T(8,128)(2,1)S(1)}, bf16[1280,5]{0,1:T(8,128)(2,1)}, u32[]{:S(2)}) copy-start(bf16[1280,5]{0,1:T(8,128)(2,1)} %param.28) | copy-start | bytes 38404
  454.0 4.7 %collective-permute-start.6 = (bf16[1,1,64,320]{3,2,1,0:T(8,128)(2,1)S(1)}, bf16[1,1,64,320]{3,2,1,0:T(8,128)(2,1)S(1)}, u32[]{:S(2)}, u32[]{:S(2)}) collective-permute-start(bf16[1,1,64,320]{3,2,1,0:T(8,128)(2,1)S(1)} %get-tuple-element.30), channel_id=1, source_target_pairs={{0,1},{1,2},{2,3},{3,4},{4,5},{5,6},{6,7},{8,9},{9,10},{10,11},{11... | collective-permute-start | bytes 122888 | tf_op jit(solution)/shard_map/ppermute | solution.py:41
  456.8 5.4 %collective-permute-start.7 = (bf16[1,1,64,320]{3,2,1,0:T(8,128)(2,1)S(1)}, bf16[1,1,64,320]{3,2,1,0:T(8,128)(2,1)S(1)}, u32[]{:S(2)}, u32[]{:S(2)}) collective-permute-start(bf16[1,1,64,320]{3,2,1,0:T(8,128)(2,1)S(1)} %get-tuple-element.31), channel_id=1, source_target_pairs={{1,0},{2,1},{3,2},{4,3},{5,4},{6,5},{7,6},{9,8},{10,9},{11,10},{12... | collective-permute-start | bytes 122888 | tf_op jit(solution)/shard_map/ppermute | solution.py:43
Sparse Core Ops, SparseCore 0:
  387.3 40.2 all-gather.1
